TPU v7x, 32 devices: a whole 2x2x4 slice. The times are simulated.
32 devices in a mesh: row: 4 (over x, core), col: 8 (over z, y).
Axes of the slice: x: 2, y: 2, z: 4, core: 2. Of those that a mesh axis runs over, the one named last changes fastest.
Arguments:
- stored: float32 [16384, 16384], P('row', 'col'), as said below
Outputs:
- updated: float32 [16384, 16384], P('row', 'col')
- log_det: float32 [], replicated
Inputs may be any that keep to these rules, and one draw needn't show every extreme that they name: `stored`: read back into global order, the matrix is symmetric positive definite, with every eigenvalue at least 1.
All inputs are finite; a program needn't handle non-finite values.
Results may differ from a plain program's by a relative error of at most 0.0001.
Values sent between devices are 32-bit elements; how exact they have to be, the bound alone decides.
A program may use at most 256 MiB of HBM per device.

v0:
```python
import jax
import jax.numpy as jnp
from jax import lax
from jax.sharding import PartitionSpec as P

NB = 512
PANELS = 2


def from_root(value, axis, source):
    kept = jnp.where(lax.axis_index(axis) == source, value, 0).astype(value.dtype)
    return lax.psum(kept, axis)


def per_device(stored):
    row_count = lax.axis_size("row")
    col_count = lax.axis_size("col")
    row_index = lax.axis_index("row")
    col_index = lax.axis_index("col")
    local_rows, local_cols = stored.shape
    ratio = col_count // row_count
    col_blocks = local_cols // NB
    row_block = jnp.arange(local_rows, dtype=jnp.int32) // NB * row_count + row_index
    col_block = jnp.arange(local_cols, dtype=jnp.int32) // NB * col_count + col_index
    identity = jnp.eye(NB, dtype=jnp.float32)
    matrix = stored
    log_total = jnp.zeros((), jnp.float32)
    for number in range(PANELS):
        own_col = number // col_count
        own_row = number // row_count
        root_row = number % row_count
        root_col = number % col_count
        column_slab = matrix[:, own_col * NB : (own_col + 1) * NB]
        pivot_block = column_slab[own_row * NB : (own_row + 1) * NB]
        pivot_block = from_root(pivot_block, ("row", "col"), root_row * col_count + root_col)
        column_slab = from_root(column_slab, "col", root_col)
        factor = jnp.linalg.cholesky(pivot_block)
        inverse = jax.scipy.linalg.solve_triangular(factor, identity, lower=True)
        solved = jnp.dot(
            column_slab,
            inverse.T,
            precision=lax.Precision.HIGHEST,
            preferred_element_type=jnp.float32,
        )
        below_mask = (row_block > number)[:, None]
        at_mask = (row_block == number)[:, None]
        tiled = jnp.tile(factor, (local_rows // NB, 1))
        panel_full = jnp.where(below_mask, solved, jnp.where(at_mask, tiled, 0.0))
        log_term = 2.0 * jnp.sum(jnp.log(jnp.diagonal(factor)))
        log_total = log_total + log_term
        picked = lax.dynamic_index_in_dim(
            panel_full.reshape(col_blocks, ratio, NB, NB), col_index // row_count, 1, keepdims=False
        )
        right_rows = from_root(picked.reshape(local_cols, NB), "row", col_index % row_count)
        left_rows = jnp.where(below_mask, panel_full, 0.0)
        right_rows = jnp.where((col_block > number)[:, None], right_rows, 0.0)
        matrix = matrix - jnp.dot(
            left_rows,
            right_rows.T,
            precision=lax.Precision.HIGHEST,
            preferred_element_type=jnp.float32,
        )
        old_column = matrix[:, own_col * NB : (own_col + 1) * NB]
        new_column = jnp.where(col_index == root_col, panel_full, old_column)
        matrix = matrix.at[:, own_col * NB : (own_col + 1) * NB].set(new_column)
        upper_mask = at_mask & (col_block > number)[None, :]
        matrix = jnp.where(upper_mask, 0.0, matrix)
    return (matrix, log_total)


def solution(mesh):
    placed = (P("row", "col"),)
    return jax.shard_map(
        per_device, mesh=mesh, in_specs=placed, out_specs=(P("row", "col"), P()), check_vma=False
    )
```

profile of v0, /device:TPU:4, one launch (start us, length us, event | category | flops | bytes accessed | tf_op | source)
XLA Modules:
  0.0 1354.7 jit_solution(7474588990909494148)
XLA Ops:
  7.2 31.1 %copy.20 = f32[4096,2048]{0,1:T(8,128)} copy(f32[4096,2048]{1,0:T(8,128)} %param.8) | data formatting | bytes 67108864 | tf_op args[0]
  38.3 2.3 slice_select_fusion.3
  40.7 7.7 slice_select_fusion.1
  48.6 124.0 %all-reduce.10.cloned.1.call-done = f32[512,512]{0,1:T(8,128)} async-done(((f32[512,512]{0,1:T(8,128)}), f32[512,512]{0,1:T(8,128)}) %all-reduce.10.cloned.1.call-update) | async-done | bytes 1048592 | tf_op jit(solution)/shard_map/psum | solution.py:12
  172.6 1.6 copy.17
  174.2 1.4 fusion.31
  175.7 11.7 cholesky.286
  187.4 9.8 custom-call.31
  199.9 11.7 cholesky.305
  211.6 10.2 custom-call.32
  223.5 11.7 cholesky.326
  235.2 9.8 custom-call.33
  246.5 11.7 cholesky.343
  264.0 11.7 while.6
  264.7 2.2 bitcast_dynamic-update-slice_fusion.4
  267.6 2.3 bitcast_dynamic-update-slice_fusion.4
  270.5 2.2 bitcast_dynamic-update-slice_fusion.4
  273.5 2.2 bitcast_dynamic-update-slice_fusion.4
  275.7 39.3 %custom-call.34 = f32[4,128,128]{1,2,0:T(8,128)S(1)} custom-call(f32[4,128,128]{2,1,0:T(8,128)S(1)} %get-tuple-element.42), custom_call_target="InvertDiagBlocksLowerTriangular" | custom-call | tf_op jit(solution)/shard_map/jit(_solve_triangular)/triangular_solve | solution.py:38
  316.4 11.3 copy.31
  331.6 1.6 convolution_subtract_fusion.7
  333.6 112.1 %all-reduce.8.cloned.1.call-done = f32[4096,512]{0,1:T(8,128)} async-done(((f32[4096,512]{0,1:T(8,128)}), f32[4096,512]{0,1:T(8,128)}) %all-reduce.8.cloned.1.call-update) | async-done | bytes 8388624 | tf_op jit(solution)/shard_map/psum | solution.py:12
  445.6 19.9 %select_select_fusion.3 = f32[4096,512]{0,1:T(8,128)} fusion(f32[4096,512]{0,1:T(8,128)} %bitcast.121, f32[4096,512]{0,1:T(8,128)} %all-reduce.8.cloned.1.call-done, pred[4096]{0:T(1024)(128)(4,1)S(1)} %get-tuple-element.97, pred[4096]{0:T(1024)(128)(4,1)S(1)} %get-tuple-element.96, f32[128,512]{1,0:T(8,128)S(1)} %fusion.78, f32[128,512]{1,0:T(8,128)S(1)} %fusion.79, ...), kind=kOutput, calls=%fused_computation.19 | convolution fusion | flops 12889882624 | bytes 26222592 | tf_op jit(solution)/shard_map/dot_general | solution.py:39
  465.5 11.7 reshape.171
  477.2 14.5 %fusion.4 = f32[4,512,512]{1,0,2:T(4,128)S(1)} fusion(pred[]{:T(512)S(6)} %eq.45, f32[4,2,512,512]{2,1,0,3:T(2,128)} %reshape.171, s32[]{:T(128)S(6)} %select_n.167), kind=kLoop, calls=%fused_computation.22 | loop fusion | flops 1048576 | bytes 8388613 | tf_op jit(solution)/shard_map/jit(_where)/select_n | solution.py:11
  491.8 3.9 copy.32
  496.6 83.9 %all-reduce.12.cloned.1.call-done = f32[2048,512]{0,1:T(8,128)} async-done(((f32[2048,512]{0,1:T(8,128)}), f32[2048,512]{0,1:T(8,128)}) %all-reduce.12.cloned.1.call-update) | async-done | bytes 4194320 | tf_op jit(solution)/shard_map/psum | solution.py:12
  580.5 60.8 %convolution_subtract_fusion.1 = f32[4096,2048]{0,1:T(8,128)} fusion(f32[4096,2048]{0,1:T(8,128)} %copy.20, f32[4096,512]{0,1:T(8,128)} %select_select_fusion.3, f32[2048,512]{0,1:T(8,128)} %all-reduce.12.cloned.1.call-done, pred[4096]{0:T(1024)(128)(4,1)S(1)} %get-tuple-element.96, pred[2048]{0:T(1024)(128)(4,1)S(1)} %fusion.103), kind=kOutput, calls=%fused_computation.9 | convolution fusion | flops 51551141888 | bytes 79697920 | tf_op jit(solution)/shard_map/dot_general | solution.py:57
  641.2 9.8 fusion
  651.0 13.1 and_select_fusion
  664.2 11.7 copy-done
  677.1 7.7 slice_select_fusion
  685.1 122.8 %all-reduce.16.cloned.1.call-done = f32[512,512]{0,1:T(8,128)} async-done(((f32[512,512]{0,1:T(8,128)}), f32[512,512]{0,1:T(8,128)}) %all-reduce.16.cloned.1.call-update) | async-done | bytes 1048592 | tf_op jit(solution)/shard_map/psum | solution.py:12
  807.9 1.6 copy.22
  809.5 1.5 fusion.30
  811.9 11.7 cholesky.358
  823.7 9.8 custom-call.35
  836.2 11.7 cholesky.377
  847.9 10.2 custom-call.36
  859.7 11.7 cholesky.398
  871.5 9.8 custom-call.37
  882.8 11.7 cholesky.415
  899.7 2.6 fusion.32
  903.7 12.0 while.7
  904.3 2.3 bitcast_dynamic-update-slice_fusion.5
  907.4 2.3 bitcast_dynamic-update-slice_fusion.5
  910.4 2.3 bitcast_dynamic-update-slice_fusion.5
  913.4 2.3 bitcast_dynamic-update-slice_fusion.5
  915.6 39.9 %custom-call.38 = f32[4,128,128]{1,2,0:T(8,128)} custom-call(f32[4,128,128]{2,1,0:T(8,128)S(1)} %get-tuple-element.43), custom_call_target="InvertDiagBlocksLowerTriangular" | custom-call | tf_op jit(solution)/shard_map/jit(_solve_triangular)/triangular_solve | solution.py:38
  955.6 2.3 tile.20
  957.9 11.3 copy.33
  973.2 1.7 convolution_subtract_fusion.6
  975.3 105.8 %all-reduce.14.cloned.1.call-done = f32[4096,512]{0,1:T(8,128)} async-done(((f32[4096,512]{0,1:T(8,128)}), f32[4096,512]{0,1:T(8,128)}) %all-reduce.14.cloned.1.call-update) | async-done | bytes 8388624 | tf_op jit(solution)/shard_map/psum | solution.py:12
  1081.2 19.7 %select_select_fusion.2 = f32[4096,512]{0,1:T(8,128)} fusion(f32[4096,512]{0,1:T(8,128)} %bitcast.122, f32[4096,512]{0,1:T(8,128)} %all-reduce.14.cloned.1.call-done, pred[4096]{0:T(1024)(128)(4,1)S(1)} %fusion.97, pred[4096]{0:T(1024)(128)(4,1)S(1)} %fusion.94, f32[128,512]{1,0:T(8,128)S(1)} %fusion.72, f32[128,512]{1,0:T(8,128)} %copy-done.5, ...), kind=kOutput, calls=%fused_computation.17 | convolution fusion | flops 12889882624 | bytes 26222592 | tf_op jit(solution)/shard_map/dot_general | solution.py:39
  1100.8 11.7 reshape.172
  1112.6 14.9 %fusion.5 = f32[4,512,512]{1,0,2:T(4,128)S(1)} fusion(pred[]{:T(512)S(6)} %eq.45, f32[4,2,512,512]{2,1,0,3:T(2,128)} %reshape.172, s32[]{:T(128)S(6)} %select_n.167), kind=kLoop, calls=%fused_computation.23 | loop fusion | flops 1048576 | bytes 8388613 | tf_op jit(solution)/shard_map/jit(_where)/select_n | solution.py:11
  1127.5 3.9 copy.34
  1131.5 4.5 gather_fusion
  1136.6 4.5 gather_fusion.1
  1143.0 73.2 %all-reduce.18.cloned.1.call-done = f32[2048,512]{0,1:T(8,128)} async-done(((f32[2048,512]{0,1:T(8,128)}), f32[2048,512]{0,1:T(8,128)}) %all-reduce.18.cloned.1.call-update) | async-done | bytes 4194320 | tf_op jit(solution)/shard_map/psum | solution.py:12
  1216.2 60.9 %convolution_subtract_fusion = f32[4096,2048]{0,1:T(8,128)} fusion(f32[4096,2048]{0,1:T(8,128)} %copy-done, f32[4096,512]{0,1:T(8,128)} %select_select_fusion.2, f32[2048,512]{0,1:T(8,128)} %all-reduce.18.cloned.1.call-done, pred[4096]{0:T(1024)(128)(4,1)S(1)} %fusion.94, pred[2048]{0:T(1024)(128)(4,1)S(1)} %fusion.104), kind=kOutput, calls=%fused_computation.8 | convolution fusion | flops 51551141888 | bytes 79697920 | tf_op jit(solution)/shard_map/dot_general | solution.py:57
  1277.1 12.2 fusion.1
  1289.3 24.0 %and_select_fusion.1 = f32[4096,2048]{0,1:T(8,128)} fusion(f32[4096,2048]{0,1:T(8,128)} %fusion.1, pred[4096]{0:T(1024)(128)(4,1)S(1)} %fusion.97, pred[2048]{0:T(1024)(128)(4,1)S(1)} %fusion.104), kind=kLoop, calls=%fused_computation.7 | loop fusion | flops 16777216 | bytes 67115008 | tf_op jit(solution)/shard_map/jit(_where)/select_n | solution.py:67
  1313.2 33.3 %copy.26 = f32[4096,2048]{1,0:T(8,128)} copy(f32[4096,2048]{0,1:T(8,128)} %and_select_fusion.1) | data formatting | bytes 67108864
  (107 shorter events, 39.1 us)
Async XLA Ops:
  7.2 165.4 %all-reduce.10.cloned.1.call-start = ((), (), s32[]{:S(2)}) async-start(), calls=%async_computation.1 | async-start | bytes 2097152 | tf_op jit(solution)/shard_map/psum | solution.py:12
  40.7 405.0 %all-reduce.8.cloned.1.call-start = ((), (), s32[]{:S(2)}) async-start(), calls=%async_computation | async-start | bytes 16777216 | tf_op jit(solution)/shard_map/psum | solution.py:12
  48.4 532.1 %all-reduce.12.cloned.1.call-start = ((), (), s32[]{:S(2)}) async-start(), calls=%async_computation.2 | async-start | bytes 8388608 | tf_op jit(solution)/shard_map/psum | solution.py:12
  175.6 11.8 copy-start.3
  495.7 312.2 %all-reduce.16.cloned.1.call-start = ((), (), s32[]{:S(2)}) async-start(), calls=%async_computation.4 | async-start | bytes 2097152 | tf_op jit(solution)/shard_map/psum | solution.py:12
  664.2 11.7 copy-start
  677.0 404.1 %all-reduce.14.cloned.1.call-start = ((), (), s32[]{:S(2)}) async-start(), calls=%async_computation.3 | async-start | bytes 16777216 | tf_op jit(solution)/shard_map/psum | solution.py:12
  684.8 531.4 %all-reduce.18.cloned.1.call-start = ((), (), s32[]{:S(2)}) async-start(), calls=%async_computation.5 | async-start | bytes 8388608 | tf_op jit(solution)/shard_map/psum | solution.py:12
  810.9 1.0 copy-start.4
  898.3 1.4 copy-start.1
  957.9 11.3 copy-start.6
  971.3 3.5 copy-start.2
  973.2 1.7 copy-start.5
Sparse Core Ops, SparseCore 0:
  40.8 131.7 all-reduce.9
  176.5 269.0 all-reduce.7
  495.8 84.6 all-reduce.11
  677.2 130.6 all-reduce.15
  811.6 269.4 all-reduce.13
  1131.6 84.5 all-reduce.17
where the time goes:
time: 1370 us; the launch traced here: 1350 us
  waiting for transfers between devices  622 us (45%)
  other arithmetic  354 us (26%)
  matrix products  184 us (13%)
  local copies, waits for them, and re-layouts  172 us (13%)
  between operations  22.2 us (2%)
    psum x6, waiting for transfers between devices, from_root(): return lax.psum(kept, axis)  622 us
    another operation x29, other arithmetic, per_device(): factor = jnp.linalg.cholesky(pivot_block)  158 us
    dot_general x2, matrix products, per_device(): jnp.dot(left_rows, right_rows.T, precision=lax.Precision.HIGHEST, preferr...  122 us
    unnamed x20, local copies, waits for them, and re-layouts  108 us
    another operation x5, other arithmetic, per_device(): inverse = jax.scipy.linalg.solve_triangular(factor, identity, lower=True)  83.1 us
    select_n x6, other arithmetic, from_root(): jnp.where(lax.axis_index(axis) == source, value, 0).astype(value.dtype)  48.3 us
    dot_general x2, matrix products, per_device(): jnp.dot(column_slab, inverse.T, precision=lax.Precision.HIGHEST, preferre...  39.5 us
    select_n x2, other arithmetic, per_device(): matrix = jnp.where(upper_mask, 0.0, matrix)  37.1 us
  transfers between devices with their start and end apart: 6, of which 6 were waited for; matrix products, arithmetic and copies ran while one was open for 26% of the time, Pallas kernels for 0%

commit v1 on v0

v1 whole, which is shorter than its diff:
```python
import functools

import jax
import jax.numpy as jnp
from jax import lax
from jax.experimental import pallas as pl
from jax.experimental.pallas import tpu as pltpu
from jax.sharding import PartitionSpec as P

NB = 512
PANELS = 2
BASE = 128
EXACT = lax.Precision.HIGHEST
SPLIT = lax.Precision.HIGH


def dot(a, b, dims, precision):
    return lax.dot_general(
        a, b, (dims, ((), ())), precision=precision, preferred_element_type=jnp.float32
    )


def factor_kernel(a_ref, l_ref, v_ref, work, aug):
    size = a_ref.shape[0]
    work[...] = a_ref[...]
    l_ref[...] = jnp.zeros_like(l_ref)
    v_ref[...] = jnp.zeros_like(v_ref)
    rows = lax.broadcasted_iota(jnp.int32, (BASE, BASE), 0)
    lanes = lax.broadcasted_iota(jnp.int32, (BASE, BASE), 1)
    row_ids = lax.broadcasted_iota(jnp.int32, (BASE, 1), 0)
    lane_ids = lax.broadcasted_iota(jnp.int32, (1, BASE), 1)
    for start in range(0, size, BASE):
        stop = start + BASE
        aug[:, :BASE] = work[start:stop, start:stop]
        aug[:, BASE:] = jnp.where(rows == lanes, 1.0, 0.0)

        def step(j, carry):
            row = aug[pl.ds(j, 1), :]
            pivot = jnp.sum(jnp.where(lane_ids == j, row[:, :BASE], 0.0), axis=1, keepdims=True)
            left = aug[:, :BASE]
            column = jnp.sum(jnp.where(lanes == j, left, 0.0), axis=1, keepdims=True)
            column = jnp.where(row_ids > j, column, 0.0)
            aug[...] = aug[...] - column * (row * (1.0 / pivot))
            return carry

        lax.fori_loop(0, BASE, step, 0)
        upper = aug[:, :BASE]
        pivots = jnp.sum(jnp.where(rows == lanes, upper, 0.0), axis=1, keepdims=True)
        scale = 1.0 / jnp.sqrt(pivots)
        lower = jnp.where(rows <= lanes, upper * scale, 0.0).T
        inverse = jnp.where(rows >= lanes, aug[:, BASE:] * scale, 0.0)
        l_ref[start:stop, start:stop] = lower
        v_ref[start:stop, start:stop] = inverse
        if start:
            mixed = dot(l_ref[start:stop, :start], v_ref[:start, :start], ((1,), (0,)), EXACT)
            v_ref[start:stop, :start] = -dot(inverse, mixed, ((1,), (0,)), EXACT)
        if stop < size:
            panel = dot(work[stop:, start:stop], inverse, ((1,), (1,)), EXACT)
            l_ref[stop:, start:stop] = panel
            work[stop:, stop:] = work[stop:, stop:] - dot(panel, panel, ((1,), (1,)), EXACT)


def factor_block(block):
    size = block.shape[0]
    shape = jax.ShapeDtypeStruct((size, size), jnp.float32)
    return pl.pallas_call(
        factor_kernel,
        out_shape=(shape, shape),
        in_specs=[pl.BlockSpec(memory_space=pltpu.VMEM)],
        out_specs=(pl.BlockSpec(memory_space=pltpu.VMEM),) * 2,
        scratch_shapes=[
            pltpu.VMEM((size, size), jnp.float32),
            pltpu.VMEM((BASE, 2 * BASE), jnp.float32),
        ],
        cost_estimate=pl.CostEstimate(
            flops=200 * 10**9 // 2, bytes_accessed=3 * 4 * size * size, transcendentals=0
        ),
    )(block)


def per_device(stored):
    row_count = lax.axis_size("row")
    col_count = lax.axis_size("col")
    row_index = lax.axis_index("row")
    col_index = lax.axis_index("col")
    local_rows, local_cols = stored.shape
    ratio = col_count // row_count
    piece = local_cols // row_count
    per_block = NB // piece
    corner = stored[:NB, :NB]

    def lead(row, col):
        return jnp.where((row_index == row) & (col_index == col), corner, 0.0)

    block00 = lax.psum(lead(0, 0), ("row", "col"))
    block1 = lax.psum(jnp.stack([lead(1, 0), lead(1, 1)]), ("row", "col"))
    block10, block11 = block1[0], block1[1]

    head = stored[:NB].reshape(NB, row_count, piece).transpose(1, 0, 2)
    swapped = lax.all_to_all(head, "row", 0, 0)
    mine = swapped[:PANELS].reshape(PANELS * NB, piece)
    pairs = []
    for q in range(row_count):
        for c in range(col_count):
            t, u = q // per_block, q % per_block
            target = (t * ratio + c // row_count) * per_block + u
            pairs.append((q * col_count + c, (c % row_count) * col_count + target))
    sent = lax.ppermute(mine, ("row", "col"), pairs)
    right_raw = lax.all_gather(mine, "row")
    left_raw = lax.all_gather(sent, "col")

    factor0, inverse0 = factor_block(block00)
    lower10 = dot(block10, inverse0, ((1,), (1,)), EXACT)
    factor1, inverse1 = factor_block(block11 - dot(lower10, lower10, ((1,), (1,)), EXACT))
    log_det = 2.0 * jnp.sum(jnp.log(jnp.diagonal(factor0)))
    log_det = log_det + 2.0 * jnp.sum(jnp.log(jnp.diagonal(factor1)))

    def solve(raw):
        raw0, raw1 = raw[:, :NB], raw[:, NB:]
        count = raw.shape[0] * raw.shape[2]
        first = jnp.einsum(
            "gkq,vk->gqv", raw0, inverse0, precision=SPLIT, preferred_element_type=jnp.float32
        ).reshape(count, NB)
        rest = raw1.transpose(0, 2, 1).reshape(count, NB) - dot(first, lower10, ((1,), (1,)), SPLIT)
        return first, dot(rest, inverse1, ((1,), (1,)), SPLIT)

    row_block = (jnp.arange(local_rows, dtype=jnp.int32) // NB * row_count + row_index)[:, None]
    left0, left1 = solve(left_raw)
    right0, right1 = solve(right_raw)
    left = jnp.concatenate([left0, left1], axis=1)
    right = jnp.concatenate([right0, right1], axis=1)
    trailing = stored - dot(left, right, ((1,), (1,)), SPLIT)
    matrix = jnp.where(row_block < PANELS, 0.0, trailing)

    tile = lambda block: jnp.tile(block, (local_rows // NB, 1))
    panel0 = jnp.where(
        row_block == 0, tile(factor0), jnp.where(row_block == 1, tile(lower10), left0)
    )
    panel1 = jnp.where(
        row_block == 0, 0.0, jnp.where(row_block == 1, tile(factor1), left1)
    )
    column = jnp.where(
        col_index == 0, panel0, jnp.where(col_index == 1, panel1, matrix[:, :NB])
    )
    return matrix.at[:, :NB].set(column), log_det


def solution(mesh):
    placed = (P("row", "col"),)
    return jax.shard_map(
        per_device, mesh=mesh, in_specs=placed, out_specs=(P("row", "col"), P()), check_vma=False
    )
```

time: 1370 us -> 851 us (0.62)
  other arithmetic: 354 us -> 30.1 us
  waiting for transfers between devices: 622 us -> 363 us
  Pallas kernels: 0 us -> 119 us
  matrix products: 184 us -> 131 us
    psum x6 -> x1, waiting for transfers between devices: 622 us -> 214 us  [per_device(): block00 = lax.psum(lead(0, 0), ('row', 'col'))]
    another operation x35 -> x3, other arithmetic: 242 us -> 4.7 us  [the longest x2 4.04 us: per_device(): block1 = lax.psum(jnp.stack([lead(1, 0), lead(1, 1)]), ('row', 'col'))]
    pallas_call x0 -> x2, Pallas kernels: none -> 119 us  [factor_block(): pl.pallas_call(factor_kernel, out_shape=(shape, shape), in_specs=[pl.Bloc...]
    ppermute x0 -> x1, waiting for transfers between devices: none -> 96.7 us  [per_device(): sent = lax.ppermute(mine, ('row', 'col'), pairs)]
    select_n x8 -> x0, other arithmetic: 85.4 us -> none  [the longest x6 48.3 us: from_root(): jnp.where(lax.axis_index(axis) == source, value, 0).astype(value.dtype)]
    all_to_all x0 -> x1, waiting for transfers between devices: none -> 52.4 us  [per_device(): swapped = lax.all_to_all(head, 'row', 0, 0)]
    dot_general x4 -> x9, matrix products: 161 us -> 131 us  [the longest x7 109 us: dot(): lax.dot_general(a, b, (dims, ((), ())), precision=precision, preferred_el...]
    transpose x0 -> x4, local copies, waits for them, and re-layouts: none -> 23.4 us  [solve(): raw1.transpose(0, 2, 1).reshape(count, NB)]
  transfers between devices with their start and end apart: 6 -> 5, of which waited for: 6 -> 3; matrix products, arithmetic and copies ran while one was open for 26% -> 17% of each run, Pallas kernels for 0% -> 14%
where the time goes in v1:
time: 851 us; the launch traced here: 844 us
  waiting for transfers between devices  363 us (43%)
  local copies, waits for them, and re-layouts  174 us (20%)
  matrix products  131 us (15%)
  Pallas kernels  119 us (14%)
  other arithmetic  30.1 us (4%)
  between operations  18.3 us (2%)
    psum x1, waiting for transfers between devices, per_device(): block00 = lax.psum(lead(0, 0), ('row', 'col'))  214 us
    pallas_call x2, Pallas kernels, factor_block(): pl.pallas_call(factor_kernel, out_shape=(shape, shape), in_specs=[pl.Bloc...  119 us
    dot_general x7, matrix products, dot(): lax.dot_general(a, b, (dims, ((), ())), precision=precision, preferred_el...  109 us
    unnamed x30, local copies, waits for them, and re-layouts  103 us
    ppermute x1, waiting for transfers between devices, per_device(): sent = lax.ppermute(mine, ('row', 'col'), pairs)  96.7 us
    all_to_all x1, waiting for transfers between devices, per_device(): swapped = lax.all_to_all(head, 'row', 0, 0)  52.4 us
    transpose x4, local copies, waits for them, and re-layouts, solve(): raw1.transpose(0, 2, 1).reshape(count, NB)  23.4 us
    scatter x1, other arithmetic, per_device(): return (matrix.at[:, :NB].set(column), log_det)  23 us
  transfers between devices with their start and end apart: 5, of which 3 were waited for; matrix products, arithmetic and copies ran while one was open for 17% of the time, Pallas kernels for 14%

profile of v1, /device:TPU:4, one launch (start us, length us, event | category | flops | bytes accessed | tf_op | source)
XLA Modules:
  0.0 843.5 jit_solution(10788579056329434477)
XLA Ops:
  8.0 4.7 slice.48
  12.7 5.4 copy.51
  18.1 4.8 all-to-all-start
  23.0 0.0 all-reduce.3.cloned.1.call-start
  23.0 2.5 select_bitcast_fusion.1
  25.5 1.5 pad_maximum_fusion
  27.1 0.0 all-reduce.3.cloned.1.call-update
  27.1 0.0 all-gather.4.cloned.1.call-start
  27.1 52.4 %all-to-all-done = f32[4,512,512]{1,2,0:T(8,128)} async-done(((f32[4,512,512]{1,2,0:T(8,128)}), f32[4,512,512]{1,2,0:T(8,128)}, u32[]{:S(2)}, u32[]{:S(2)}) %all-to-all-start) | async-done | bytes 4194336 | tf_op jit(solution)/shard_map/all_to_all | solution.py:100
  79.6 1.8 slice.61
  81.4 1.9 copy.67
  83.3 0.0 all-gather.4.cloned.1.call-update
  83.3 0.0 all-gather.6.cloned.1.call-start
  83.3 2.4 collective-permute-start
  85.8 96.7 %collective-permute-done = f32[1024,512]{1,0:T(8,128)S(1)} collective-permute-done((f32[1024,512]{1,0:T(8,128)}, f32[1024,512]{1,0:T(8,128)S(1)}, u32[]{:S(2)}, u32[]{:S(2)}) %collective-permute-start) | collective-permute-done | bytes 2097184 | tf_op jit(solution)/shard_map/ppermute | solution.py:108
  182.5 1.4 copy-done.7
  183.8 0.0 all-gather.6.cloned.1.call-update
  183.9 31.6 %copy.59 = f32[4096,2048]{0,1:T(8,128)} copy(f32[4096,2048]{1,0:T(8,128)} %param.3) | data formatting | bytes 67108864 | tf_op args[0]
  215.4 0.7 compare_reduce_fusion
  216.1 0.6 shift-left_or_fusion
  216.7 0.6 fusion.19
  217.3 0.6 fusion.17
  217.9 214.0 %all-reduce.3.cloned.1.call-done = (f32[512,512]{1,0:T(8,128)}, f32[2,512,512]{2,1,0:T(8,128)}) async-done(((f32[512,512]{1,0:T(8,128)}, f32[2,512,512]{2,1,0:T(8,128)}), (f32[512,512]{1,0:T(8,128)}, f32[2,512,512]{2,1,0:T(8,128)})) %all-reduce.3.cloned.1.call-update) | async-done | bytes 3145744 | tf_op jit(solution)/shard_map/psum | solution.py:95
  431.9 59.5 %shard_map.30 = (f32[512,512]{1,0:T(8,128)}, f32[512,512]{1,0:T(8,128)}) custom-call(f32[512,512]{1,0:T(8,128)} %get-tuple-element.32.a_ref), custom_call_target="tpu_custom_call" | custom-call | flops 99999997952 | bytes 3145728 | tf_op jit(solution)/shard_map/pallas_call | solution.py:66
  491.4 0.0 copy-done.8
  491.4 3.1 fusion.10
  494.5 0.3 copy.62
  494.9 4.1 convolution_subtract_fusion.a_ref
  498.9 59.4 %shard_map.31 = (f32[512,512]{1,0:T(8,128)}, f32[512,512]{1,0:T(8,128)}) custom-call(f32[512,512]{1,0:T(8,128)} %convolution_subtract_fusion.a_ref), custom_call_target="tpu_custom_call" | custom-call | flops 99999997952 | bytes 3145728 | tf_op jit(solution)/shard_map/pallas_call | solution.py:66
  558.4 2.5 copy.64
  560.9 0.0 copy-done.4
  560.9 1.3 copy.61
  562.3 8.5 %gather_fusion.1 = f32[512]{0:T(512)S(1)} fusion(f32[512,512]{1,0:T(8,128)} %get-tuple-element.21, s32[512]{0:T(512)S(1)} %bitcast.60), kind=kCustom, calls=%fused_computation.1 | custom fusion | bytes 8192 | tf_op jit(solution)/shard_map/jit(diagonal)/cond/branch_0_fun/gather | solution.py:116
  570.7 4.7 gather_fusion
  575.4 2.3 tile.31
  577.7 11.3 %copy.72 = f32[64,8,8,512]{3,1,2,0:T(8,128)} copy(f32[64,8,8,512]{3,2,1,0:T(8,128)S(1)} %bitcast.66) | data formatting | bytes 16777216
  589.1 1.1 tile.14
  590.1 11.6 %copy.71 = f32[64,8,8,512]{3,1,2,0:T(8,128)} copy(f32[64,8,8,512]{3,2,1,0:T(8,128)S(1)} %bitcast.67) | data formatting | bytes 16777216
  601.7 1.1 tile.12
  602.8 11.7 %copy.70 = f32[64,8,8,512]{3,1,2,0:T(8,128)} copy(f32[64,8,8,512]{3,2,1,0:T(8,128)S(1)} %bitcast.68) | data formatting | bytes 16777216
  614.6 0.6 log_reduce_fusion
  616.4 0.0 all-gather.4.cloned.1.call-done
  616.5 4.7 slice_bitcast_fusion.1
  621.1 5.3 copy.57
  626.4 10.5 %fusion.8 = f32[512,4,512]{0,2,1:T(8,128)} fusion(f32[4,1024,512]{2,1,0:T(8,128)} %all-gather.4.cloned.1.call-done, f32[512,512]{1,0:T(8,128)S(1)} %copy-done.3), kind=kOutput, calls=%fused_computation.15 | convolution fusion | flops 3221225472 | bytes 9437184 | tf_op jit(solution)/shard_map/gkq,vk->gqv/dot_general | solution.py:121
  636.9 5.4 copy.58
  642.3 8.2 bitcast_subtract_fusion.1
  650.5 0.0 copy-done.5
  650.6 5.3 fusion.23
  655.9 11.3 %fusion.3 = f32[512,8,512]{0,2,1:T(8,128)} fusion(f32[8,1024,512]{2,1,0:T(8,128)} %bitcast.72, f32[512,512]{1,0:T(8,128)S(1)} %copy-done.3), kind=kOutput, calls=%fused_computation.7 | convolution fusion | flops 6442450944 | bytes 17825792 | tf_op jit(solution)/shard_map/gkq,vk->gqv/dot_general | solution.py:121
  667.2 4.3 slice_bitcast_fusion
  671.5 9.1 %copy.54 = f32[8,512,512]{2,1,0:T(8,128)} copy(f32[8,512,512]{1,2,0:T(8,128)} %slice_bitcast_fusion) | data formatting | bytes 16777216 | tf_op jit(solution)/shard_map/transpose | solution.py:124
  680.6 8.9 %copy.55 = f32[4096,512]{0,1:T(8,128)} copy(f32[4096,512]{1,0:T(8,128)} %bitcast.62) | data formatting | bytes 16777216 | tf_op jit(solution)/shard_map/reshape | solution.py:123
  689.6 10.7 %bitcast_subtract_fusion = f32[4096,512]{1,0:T(8,128)S(1)} fusion(f32[8,512,512]{2,1,0:T(8,128)} %copy.54, f32[4096,512]{1,0:T(8,128)} %bitcast.63, f32[512,512]{1,0:T(8,128)S(1)} %fusion.10), kind=kOutput, calls=%fused_computation.12 | convolution fusion | flops 6444548096 | bytes 26214400 | tf_op jit(solution)/shard_map/dot_general | solution.py:18
  700.3 7.1 fusion.22
  707.4 0.0 copy-done.11
  707.4 0.0 copy-start.1
  707.4 0.0 copy-start.9
  707.4 0.0 copy-start.10
  707.4 70.9 %subtract_select_fusion = f32[4096,2048]{0,1:T(8,128)} fusion(f32[4096,2048]{0,1:T(8,128)} %copy.59, f32[4096,512]{0,1:T(8,128)S(1)} %fusion.22, f32[4096,512]{0,1:T(8,128)} %copy.55, pred[4096]{0:T(1024)(128)(4,1)S(1)} %copy-done.11, f32[2048,512]{0,1:T(8,128)} %fusion.23, f32[2048,512]{0,1:T(8,128)} %copy.58), kind=kOutput, calls=%fused_computation.2 | convolution fusion | flops 51562676224 | bytes 92278784 | tf_op jit(solution)/shard_map/dot_general | solution.py:18
  778.3 0.0 copy-done.9
  778.3 0.0 copy-done.10
  778.3 23.0 %select_dynamic-update-slice_fusion = f32[4096,2048]{0,1:T(8,128)} fusion(f32[4096,2048]{0,1:T(8,128)} %subtract_select_fusion, f32[4096,512]{0,1:T(8,128)} %bitcast.69, f32[4096,512]{0,1:T(8,128)} %copy-done.1, f32[4096,512]{0,1:T(8,128)} %bitcast.71, f32[4096,512]{0,1:T(8,128)} %bitcast.70, f32[4096,512]{0,1:T(8,128)} %copy.55, pred[]{:T(512)S(6)} %eq.37, ...), kind=kLoop, calls=%fused_computation.13 | loop fusion | flops 14680064 | bytes 58728960 | tf_op jit(solution)/shard_map/scatter | solution.py:145
  801.4 33.3 %copy.65 = f32[4096,2048]{1,0:T(8,128)} copy(f32[4096,2048]{0,1:T(8,128)} %select_dynamic-update-slice_fusion) | data formatting | bytes 67108864
  (15 shorter events, 0.0 us)
Async XLA Ops:
  18.1 61.5 %all-to-all-start = ((f32[4,512,512]{1,2,0:T(8,128)}), f32[4,512,512]{1,2,0:T(8,128)}, u32[]{:S(2)}, u32[]{:S(2)}) async-start(f32[4,512,512]{1,2,0:T(8,128)} %bitcast.74), calls=%async_computation | async-start | bytes 8388608 | tf_op jit(solution)/shard_map/all_to_all | solution.py:100
  23.0 409.0 %all-reduce.3.cloned.1.call-start = ((), (), s32[]{:S(2)}) async-start(), calls=%async_computation.3 | async-start | bytes 6291456 | tf_op jit(solution)/shard_map/psum | solution.py:95
  27.1 589.3 %all-gather.4.cloned.1.call-start = ((), (), s32[]{:S(2)}) async-start(), calls=%async_computation.1 | async-start | bytes 10485760 | tf_op jit(solution)/shard_map/all_gather | solution.py:109
  83.3 572.6 %all-gather.6.cloned.1.call-start = ((), (), s32[]{:S(2)}) async-start(), calls=%async_computation.2 | async-start | bytes 18874368 | tf_op jit(solution)/shard_map/all_gather | solution.py:110
  83.3 99.1 %collective-permute-start = (f32[1024,512]{1,0:T(8,128)}, f32[1024,512]{1,0:T(8,128)S(1)}, u32[]{:S(2)}, u32[]{:S(2)}) collective-permute-start(f32[1024,512]{1,0:T(8,128)} %bitcast.76), channel_id=1, source_target_pairs={{0,0},{1,8},{2,16},{3,24},{4,1},{5,9},{6,17},{7,25},{8,2},{9,10},{... | collective-permute-start | bytes 6291464 | tf_op jit(solution)/shard_map/ppermute | solution.py:108
  182.5 1.4 copy-start.7
  431.9 59.5 %copy-start.8 = (f32[2,512,512]{2,1,0:T(8,128)S(1)}, f32[2,512,512]{2,1,0:T(8,128)}, u32[]{:S(2)}) copy-start(f32[2,512,512]{2,1,0:T(8,128)} %get-tuple-element.33) | copy-start | bytes 6291460
  498.9 62.0 %copy-start.4 = (f32[512,512]{1,0:T(8,128)S(1)}, f32[512,512]{1,0:T(8,128)}, u32[]{:S(2)}) copy-start(f32[512,512]{1,0:T(8,128)} %get-tuple-element.20) | copy-start | bytes 3145732
  498.9 63.3 %copy-start = (s32[512,1]{0,1:T(1,128)S(1)}, s32[512,1]{0,1:T(1,128)}, u32[]{:S(2)}) copy-start(s32[512,1]{0,1:T(1,128)} %shift-left_or_fusion) | copy-start | bytes 6148
  590.1 11.6 %copy-start.6 = (f32[512,512]{0,1:T(8,128)S(1)}, f32[512,512]{0,1:T(8,128)}, u32[]{:S(2)}) copy-start(f32[512,512]{0,1:T(8,128)} %copy.61) | copy-start | bytes 3145732
  616.4 10.0 %copy-start.3 = (f32[512,512]{1,0:T(8,128)S(1)}, f32[512,512]{1,0:T(8,128)}, u32[]{:S(2)}) copy-start(f32[512,512]{1,0:T(8,128)} %get-tuple-element.18) | copy-start | bytes 3145732
  642.3 8.3 copy-start.5
  655.9 11.3 %copy-start.2 = (f32[8192,512]{1,0:T(8,128)S(1)}, f32[8192,512]{1,0:T(8,128)}, u32[]{:S(2)}) copy-start(f32[8192,512]{1,0:T(8,128)} %all-gather.6.cloned.1.call-done) | copy-start | bytes 50331652
  700.3 7.1 copy-start.11
  707.4 70.9 %copy-start.1 = (f32[4096,512]{0,1:T(8,128)}, f32[4096,512]{0,1:T(8,128)S(1)}, u32[]{:S(2)}) copy-start(f32[4096,512]{0,1:T(8,128)S(1)} %fusion.22) | copy-start | bytes 25165828
  707.4 70.9 %copy-start.9 = (pred[4096]{0:T(1024)(128)(4,1)S(1)}, pred[4096]{0:T(1024)(128)(4,1)}, u32[]{:S(2)}) copy-start(pred[4096]{0:T(1024)(128)(4,1)} %get-tuple-element.37) | copy-start | bytes 12292
  707.4 70.9 %copy-start.10 = (pred[4096]{0:T(1024)(128)(4,1)S(1)}, pred[4096]{0:T(1024)(128)(4,1)}, u32[]{:S(2)}) copy-start(pred[4096]{0:T(1024)(128)(4,1)} %get-tuple-element.38) | copy-start | bytes 12292
Sparse Core Ops, SparseCore 0:
  29.5 402.3 all-reduce.2
Sparse Core Ops, SparseCore 1:
  83.4 94.7 all-gather.3
  183.9 232.6 all-gather.5
